TPU v7x, 32 devices: a whole 2x2x4 slice. The times are simulated.
32 devices in a mesh: section: 8 (over y, x, core), tensor: 4 (over z).
Axes of the slice: x: 2, y: 2, z: 4, core: 2. Of those that a mesh axis runs over, the one named last changes fastest.
Arguments:
- key_weight: bfloat16 [8, 8192, 1024], P('section', None, 'tensor'), may hold values from -0.0625 to 0.0625
- value_weight: bfloat16 [8, 8192, 1024], P('section', None, 'tensor'), may hold values from -0.0625 to 0.0625
- norm_gain: bfloat16 [8, 8192], P('section'), may hold values from 0.25 to 1.75
Outputs:
- scaled: bfloat16 [8, 8192, 2048], P(None, ('section', 'tensor'))
- block_scale: float32 [8, 64, 16], P(None, 'section')
All inputs are finite; a program needn't handle non-finite values.
Results may differ from a plain program's by a relative error of at most 0.0056.
Values may be sent and summed in bfloat16 or wider, within the bound.
No kernel may reach another device: no remote copies, remote signals or barrier semaphores. Data moves between devices by JAX's collectives and lax.ppermute only.
A program may use at most 128 MiB of HBM per device.

v0:
```python
import functools

import jax
import jax.numpy as jnp
from jax import lax
from jax.experimental import pallas as pl
from jax.experimental.pallas import tpu as pltpu
from jax.sharding import PartitionSpec as P


BLOCK = 128
AXES = ("section", "tensor")

scale_floor = 0.00390625


def partner(index, step, count):
    if count & (count - 1) == 0:
        return index ^ step
    return (index + step) % count


def origin(index, step, count):
    if count & (count - 1) == 0:
        return index ^ step
    return (index + count - step) % count


def column_gain(gain):
    return jnp.broadcast_to(gain, (BLOCK, BLOCK)).T


def fold(weight, gain):
    return (weight.astype(jnp.float32) * gain).astype(jnp.bfloat16).astype(jnp.float32)


def block_max(folded):
    largest = jnp.max(jnp.max(jnp.abs(folded), axis=0, keepdims=True), axis=1, keepdims=True)
    return jnp.maximum(largest, scale_floor)


def pack_kernel(
    steps, sections_count, ranks_count, shares, key_ref, value_ref, gain_ref, out_ref, raw, gain, sems
):
    section = lax.axis_index("section")
    rank = lax.axis_index("tensor")
    rows, head_cols = raw.shape[1:]
    to_section = partner(section, steps[0], sections_count)
    to_unit = partner(rank // shares, steps[1], ranks_count // shares)
    first = pl.multiple_of((to_section * (ranks_count // shares) + to_unit) * rows, rows)
    copies = [
        pltpu.make_async_copy(key_ref.at[0, pl.ds(first, rows)], raw.at[0], sems.at[0]),
        pltpu.make_async_copy(value_ref.at[0, pl.ds(first, rows)], raw.at[1], sems.at[1]),
        pltpu.make_async_copy(gain_ref.at[:, pl.ds(first, rows)], gain, sems.at[2]),
    ]
    for copy in copies:
        copy.start()
    for copy in reversed(copies):
        copy.wait()
    share_rows = rows // shares
    for row in range(0, rows, BLOCK):
        gains = column_gain(gain[:, row : row + BLOCK].astype(jnp.float32))
        for kind in range(2):
            for col in range(0, head_cols, BLOCK):
                folded = fold(raw[kind, row : row + BLOCK, col : col + BLOCK], gains)
                scaled = (folded / block_max(folded)).astype(jnp.bfloat16)
                to = kind * head_cols + col
                if shares == 1:
                    out_ref[0, row : row + BLOCK, to : to + BLOCK] = scaled
                    continue
                for part in range(BLOCK // share_rows):
                    place = origin(row // share_rows + part, rank % shares, shares)
                    out_ref[place, :, to : to + BLOCK] = scaled[
                        part * share_rows : (part + 1) * share_rows
                    ]


def pack(steps, sections_count, ranks_count, weights):
    key_weight, value_weight, norm_gain = weights
    model_rows, head_cols = key_weight.shape[1:]
    row_share = model_rows // (sections_count * ranks_count)
    shares = max(1, BLOCK // row_share)
    rows = row_share * shares
    any_ref = pl.BlockSpec(memory_space=pl.ANY)
    return pl.pallas_call(
        functools.partial(pack_kernel, steps, sections_count, ranks_count, shares),
        out_shape=jax.ShapeDtypeStruct((shares, row_share, 2 * head_cols), jnp.bfloat16),
        in_specs=[any_ref] * 3,
        out_specs=pl.BlockSpec(memory_space=pltpu.VMEM),
        scratch_shapes=[
            pltpu.VMEM((2, rows, head_cols), jnp.bfloat16),
            pltpu.VMEM((1, rows), jnp.bfloat16),
            pltpu.SemaphoreType.DMA((3,)),
        ],
        compiler_params=pltpu.CompilerParams(vmem_limit_bytes=60 * 2**20),
        cost_estimate=pl.CostEstimate(
            flops=rows * head_cols * 40, bytes_accessed=rows * head_cols * 8, transcendentals=0
        ),
        name="pack",
    )(key_weight, value_weight, norm_gain)


def place_kernel(steps, sections_count, ranks_count, has_out, *refs):
    blocks = refs[: len(steps)]
    out_ref, sems = refs[len(steps) + has_out :]
    section = lax.axis_index("section")
    rank = lax.axis_index("tensor")
    head_cols = blocks[0].shape[1] // 2
    copies = []
    for index, (far, near) in enumerate(steps):
        layer = origin(section, far, sections_count)
        head = origin(rank, near, ranks_count)
        for kind in range(2):
            first = pl.multiple_of((kind * ranks_count + head) * head_cols, head_cols)
            copies.append(
                pltpu.make_async_copy(
                    blocks[index].at[:, pl.ds(kind * head_cols, head_cols)],
                    out_ref.at[layer, :, pl.ds(first, head_cols)],
                    sems.at[2 * index + kind],
                )
            )
    for copy in copies:
        copy.start()
    for copy in copies:
        copy.wait()


def place(steps, sections_count, ranks_count, blocks, out):
    rows, cols = blocks[0].shape
    shape = jax.ShapeDtypeStruct((sections_count, rows, ranks_count * cols), jnp.bfloat16)
    has_out = 0 if out is None else 1
    any_ref = pl.BlockSpec(memory_space=pl.ANY)
    return pl.pallas_call(
        functools.partial(place_kernel, steps, sections_count, ranks_count, has_out),
        out_shape=shape,
        in_specs=[pl.BlockSpec(memory_space=pltpu.VMEM)] * len(blocks) + [any_ref] * has_out,
        out_specs=any_ref,
        scratch_shapes=[pltpu.SemaphoreType.DMA((2 * len(steps),))],
        input_output_aliases={len(blocks): 0} if has_out else {},
        compiler_params=pltpu.CompilerParams(vmem_limit_bytes=4 * 2**20),
        cost_estimate=pl.CostEstimate(
            flops=len(steps) * rows * cols, bytes_accessed=len(steps) * rows * cols * 4, transcendentals=0
        ),
        name="place",
    )(*blocks, *([] if out is None else [out]))


def scales_kernel(key_ref, value_ref, gain_ref, out_ref):
    rows, head_cols = key_ref.shape[1:]
    ranks_count = out_ref.shape[1]
    rank = lax.axis_index("tensor")
    cols_here = head_cols // BLOCK
    shape = (rows // BLOCK, BLOCK)
    row_of = lax.broadcasted_iota(jnp.int32, shape, 0)
    lane_of = lax.broadcasted_iota(jnp.int32, shape, 1)
    found = jnp.zeros(shape, jnp.float32)
    for row in range(rows // BLOCK):
        span = slice(row * BLOCK, (row + 1) * BLOCK)
        gains = column_gain(gain_ref[:, span].astype(jnp.float32))
        for kind, ref in enumerate((key_ref, value_ref)):
            for col in range(cols_here):
                folded = fold(ref[0, span, col * BLOCK : (col + 1) * BLOCK], gains)
                lane = (kind * ranks_count + rank) * cols_here + col
                here = jnp.logical_and(row_of == row, lane_of == lane)
                found = jnp.where(here, block_max(folded), found)
    for copy in range(ranks_count):
        out_ref[0, copy] = found.astype(jnp.bfloat16)


def scales(sections_count, ranks_count, weights):
    key_weight, value_weight, norm_gain = weights
    model_rows, head_cols = key_weight.shape[1:]
    rows = model_rows // sections_count
    weight_spec = pl.BlockSpec((1, rows, head_cols), lambda i: (0, i, 0))
    return pl.pallas_call(
        scales_kernel,
        grid=(sections_count,),
        out_shape=jax.ShapeDtypeStruct(
            (sections_count, ranks_count, rows // BLOCK, BLOCK), jnp.bfloat16
        ),
        in_specs=[weight_spec, weight_spec, pl.BlockSpec((1, rows), lambda i: (0, i))],
        out_specs=pl.BlockSpec((1, ranks_count, rows // BLOCK, BLOCK), lambda i: (i, 0, 0, 0)),
        compiler_params=pltpu.CompilerParams(vmem_limit_bytes=60 * 2**20),
        cost_estimate=pl.CostEstimate(
            flops=model_rows * head_cols * 20, bytes_accessed=model_rows * head_cols * 4, transcendentals=0
        ),
        name="scales",
    )(key_weight, value_weight, norm_gain)


def send_order(sections_count, units_count):
    half = units_count // 2
    far_steps = [(far, unit) for far in range(sections_count) for unit in reversed(range(half, units_count))]
    near_steps = [(far, unit) for far in range(sections_count) for unit in reversed(range(half))]
    near_steps = near_steps[half:] + near_steps[:half]
    order = far_steps[:2]
    for index, step in enumerate(far_steps[2:]):
        order += near_steps[index : index + 1] + [step]
    rest = near_steps[len(far_steps) - 2 :]
    return order[:2] + rest[:-1] + order[2:] + rest[-1:]


def on_device(key_weight, value_weight, norm_gain):
    sections_count = lax.axis_size("section")
    ranks_count = lax.axis_size("tensor")
    sizes = (sections_count, ranks_count)
    weights = (key_weight, value_weight, norm_gain)
    model_rows, head_cols = key_weight.shape[1:]
    row_share = model_rows // (sections_count * ranks_count)
    shares = max(1, BLOCK // row_share)
    order = send_order(sections_count, ranks_count // shares)
    arrived = {}
    for far, unit in order:
        packed = pack((far, unit), *sizes, weights)
        for part in range(shares):
            near = unit * shares + part
            pairs = [
                (
                    section * ranks_count + rank,
                    partner(section, far, sections_count) * ranks_count
                    + partner(rank, near, ranks_count),
                )
                for section in range(sections_count)
                for rank in range(ranks_count)
            ]
            block = packed[part]
            if (far, near) != (0, 0):
                block = lax.ppermute(block, AXES, pairs)
            arrived[far, near] = block
    sent_scales = scales(*sizes, weights)
    got = lax.all_to_all(
        sent_scales.reshape((sections_count * ranks_count,) + sent_scales.shape[2:]), AXES, 0, 0, tiled=True
    )
    col_blocks = 2 * ranks_count * head_cols // BLOCK
    block_scale = jnp.max(got.reshape(sent_scales.shape), axis=1)[:, :, :col_blocks].astype(jnp.float32)
    last = tuple(unit * shares + shares - 1 if i else unit for i, unit in enumerate(order[-2]))
    out = None
    groups = [[(far, near) for near in range(ranks_count) if (far, near) != last] for far in range(sections_count)]
    for steps in groups + [[last]]:
        out = place(steps, *sizes, [arrived[step] for step in steps], out)
    return (out, block_scale)


def solution(mesh):
    placed = (P("section", None, "tensor"), P("section", None, "tensor"), P("section", None))

    return jax.shard_map(
        on_device,
        mesh=mesh,
        in_specs=placed,
        out_specs=(P(None, AXES, None), P(None, "section", None)),
        check_vma=False,
    )
```

profile of v0, /device:TPU:0, one launch (start us, length us, event | category | flops | bytes accessed | tf_op | source)
XLA Modules:
  0.0 227.9 jit_solution(17311669896909984986)
XLA Ops:
  2.6 3.1 %collective-permute-start.28 = (bf16[256,512]{1,0:T(8,128)(2,1)}, bf16[256,512]{1,0:T(8,128)(2,1)S(1)}, u32[]{:S(2)}, u32[]{:S(2)}) collective-permute-start(bf16[256,512]{1,0:T(8,128)(2,1)} %bitcast.56), channel_id=1, source_target_pairs={{0,1},{1,0},{2,3},{3,2},{4,5},{5,4},{6,7},{7,6},{8,9},{9,8},{10,11... | collective-permute-start | bytes 786440 | tf_op jit(solution)/shard_map/ppermute | solution.py:228
  7.7 2.7 %collective-permute-start.29 = (bf16[256,512]{1,0:T(8,128)(2,1)}, bf16[256,512]{1,0:T(8,128)(2,1)S(1)}, u32[]{:S(2)}, u32[]{:S(2)}) collective-permute-start(bf16[256,512]{1,0:T(8,128)(2,1)} %bitcast.55), channel_id=1, source_target_pairs={{0,2},{1,3},{2,0},{3,1},{4,6},{5,7},{6,4},{7,5},{8,10},{9,11},{10,... | collective-permute-start | bytes 786440 | tf_op jit(solution)/shard_map/ppermute | solution.py:228
  14.5 2.0 pack.57
  19.5 3.2 %collective-permute-start.26 = (bf16[256,512]{1,0:T(8,128)(2,1)}, bf16[256,512]{1,0:T(8,128)(2,1)S(1)}, u32[]{:S(2)}, u32[]{:S(2)}) collective-permute-start(bf16[256,512]{1,0:T(8,128)(2,1)} %bitcast.51), channel_id=1, source_target_pairs={{0,6},{1,7},{2,4},{3,5},{4,2},{5,3},{6,0},{7,1},{8,14},{9,15},{10,... | collective-permute-start | bytes 786440 | tf_op jit(solution)/shard_map/ppermute | solution.py:228
  26.7 2.0 pack.53
  28.7 2.1 pack.54
  30.8 2.0 pack.55
  34.8 13.4 %collective-permute-start.21 = (bf16[256,512]{1,0:T(8,128)(2,1)S(1)}, bf16[256,512]{1,0:T(8,128)(2,1)S(1)}, u32[]{:S(2)}, u32[]{:S(2)}) collective-permute-start(bf16[256,512]{1,0:T(8,128)(2,1)S(1)} %bitcast.44), channel_id=1, source_target_pairs={{0,9},{1,8},{2,11},{3,10},{4,13},{5,12},{6,15},{7,14},{8,1},{9,0},... | collective-permute-start | bytes 786440 | tf_op jit(solution)/shard_map/ppermute | solution.py:228
  49.2 3.5 %collective-permute-start.23 = (bf16[256,512]{1,0:T(8,128)(2,1)}, bf16[256,512]{1,0:T(8,128)(2,1)S(1)}, u32[]{:S(2)}, u32[]{:S(2)}) collective-permute-start(bf16[256,512]{1,0:T(8,128)(2,1)} %bitcast.39), channel_id=1, source_target_pairs={{0,11},{1,10},{2,9},{3,8},{4,15},{5,14},{6,13},{7,12},{8,3},{9,2},... | collective-permute-start | bytes 786440 | tf_op jit(solution)/shard_map/ppermute | solution.py:228
  58.7 2.1 pack.51
  62.7 5.0 %collective-permute-start.16 = (bf16[256,512]{1,0:T(8,128)(2,1)}, bf16[256,512]{1,0:T(8,128)(2,1)S(1)}, u32[]{:S(2)}, u32[]{:S(2)}) collective-permute-start(bf16[256,512]{1,0:T(8,128)(2,1)} %bitcast.16), channel_id=1, source_target_pairs={{0,12},{1,13},{2,14},{3,15},{4,8},{5,9},{6,10},{7,11},{8,4},{9,5},... | collective-permute-start | bytes 786440 | tf_op jit(solution)/shard_map/ppermute | solution.py:228
  70.7 4.6 %collective-permute-done.22.refs_2_ = bf16[256,512]{1,0:T(8,128)(2,1)S(1)} collective-permute-done((bf16[256,512]{1,0:T(8,128)(2,1)S(1)}, bf16[256,512]{1,0:T(8,128)(2,1)S(1)}, u32[]{:S(2)}, u32[]{:S(2)}) %collective-permute-start.22) | collective-permute-done | bytes 262176 | tf_op jit(solution)/shard_map/ppermute | solution.py:228
  80.8 2.0 pack.47
  86.8 21.6 %collective-permute-start.13 = (bf16[256,512]{1,0:T(8,128)(2,1)}, bf16[256,512]{1,0:T(8,128)(2,1)S(1)}, u32[]{:S(2)}, u32[]{:S(2)}) collective-permute-start(bf16[256,512]{1,0:T(8,128)(2,1)} %bitcast.50), channel_id=1, source_target_pairs={{0,17},{1,16},{2,19},{3,18},{4,21},{5,20},{6,23},{7,22},{8,25},{9,... | collective-permute-start | bytes 786440 | tf_op jit(solution)/shard_map/ppermute | solution.py:228
  108.7 3.2 %collective-permute-start.15 = (bf16[256,512]{1,0:T(8,128)(2,1)}, bf16[256,512]{1,0:T(8,128)(2,1)}, u32[]{:S(2)}, u32[]{:S(2)}) collective-permute-start(bf16[256,512]{1,0:T(8,128)(2,1)} %bitcast.45), channel_id=1, source_target_pairs={{0,19},{1,18},{2,17},{3,16},{4,23},{5,22},{6,21},{7,20},{8,27},{9,... | collective-permute-start | bytes 786440 | tf_op jit(solution)/shard_map/ppermute | solution.py:228
  111.9 2.3 %collective-permute-start.10 = (bf16[256,512]{1,0:T(8,128)(2,1)}, bf16[256,512]{1,0:T(8,128)(2,1)}, u32[]{:S(2)}, u32[]{:S(2)}) collective-permute-start(bf16[256,512]{1,0:T(8,128)(2,1)} %bitcast.43), channel_id=1, source_target_pairs={{0,22},{1,23},{2,20},{3,21},{4,18},{5,19},{6,16},{7,17},{8,30},{9,... | collective-permute-start | bytes 786440 | tf_op jit(solution)/shard_map/ppermute | solution.py:228
  123.8 2.0 pack.38
  126.5 2.2 collective-permute-start.8
  128.7 9.1 %collective-permute-done.14.refs_2_ = bf16[256,512]{1,0:T(8,128)(2,1)S(1)} collective-permute-done((bf16[256,512]{1,0:T(8,128)(2,1)}, bf16[256,512]{1,0:T(8,128)(2,1)S(1)}, u32[]{:S(2)}, u32[]{:S(2)}) %collective-permute-start.14) | collective-permute-done | bytes 262176 | tf_op jit(solution)/shard_map/ppermute | solution.py:228
  138.6 4.1 %collective-permute-done.10.refs_2_ = bf16[256,512]{1,0:T(8,128)(2,1)} collective-permute-done((bf16[256,512]{1,0:T(8,128)(2,1)}, bf16[256,512]{1,0:T(8,128)(2,1)}, u32[]{:S(2)}, u32[]{:S(2)}) %collective-permute-start.10) | collective-permute-done | bytes 262176 | tf_op jit(solution)/shard_map/ppermute | solution.py:228
  142.7 7.3 %collective-permute-start.5 = (bf16[256,512]{1,0:T(8,128)(2,1)}, bf16[256,512]{1,0:T(8,128)(2,1)}, u32[]{:S(2)}, u32[]{:S(2)}) collective-permute-start(bf16[256,512]{1,0:T(8,128)(2,1)} %bitcast.5), channel_id=1, source_target_pairs={{0,25},{1,24},{2,27},{3,26},{4,29},{5,28},{6,31},{7,30},{8,17},{9,... | collective-permute-start | bytes 786440 | tf_op jit(solution)/shard_map/ppermute | solution.py:228
  150.1 9.1 %collective-permute-start.6 = (bf16[256,512]{1,0:T(8,128)(2,1)}, bf16[256,512]{1,0:T(8,128)(2,1)}, u32[]{:S(2)}, u32[]{:S(2)}) collective-permute-start(bf16[256,512]{1,0:T(8,128)(2,1)} %bitcast.38), channel_id=1, source_target_pairs={{0,26},{1,27},{2,24},{3,25},{4,30},{5,31},{6,28},{7,29},{8,18},{9,... | collective-permute-start | bytes 786440 | tf_op jit(solution)/shard_map/ppermute | solution.py:228
  159.2 8.3 %scales.1 = bf16[8,4,8,128]{3,2,1,0:T(8,128)(2,1)} custom-call(bf16[1,8192,256]{2,1,0:T(8,128)(2,1)} %key_ref.65, bf16[1,8192,256]{2,1,0:T(8,128)(2,1)} %value_ref.65, bf16[1,8192]{1,0:T(2,128)(2,1)} %gain_ref.65), custom_call_target="tpu_custom_call" | custom-call | flops 41943040 | bytes 8388608 | tf_op jit(solution)/shard_map/scales/pallas_call | solution.py:175
  167.5 5.0 %all-to-all-start = ((bf16[32,8,128]{2,1,0:T(8,128)(2,1)}), bf16[32,8,128]{2,1,0:T(8,128)(2,1)S(1)}, u32[]{:S(2)}, u32[]{:S(2)}) async-start(bf16[32,8,128]{2,1,0:T(8,128)(2,1)} %bitcast.36), calls=%async_computation | async-start | bytes 131072 | tf_op jit(solution)/shard_map/all_to_all | solution.py:231
  180.5 2.0 pack.35
  184.6 5.5 %collective-permute-start.7 = (bf16[256,512]{1,0:T(8,128)(2,1)}, bf16[256,512]{1,0:T(8,128)(2,1)}, u32[]{:S(2)}, u32[]{:S(2)}) collective-permute-start(bf16[256,512]{1,0:T(8,128)(2,1)} %bitcast.7), channel_id=1, source_target_pairs={{0,27},{1,26},{2,25},{3,24},{4,31},{5,30},{6,29},{7,28},{8,19},{9,... | collective-permute-start | bytes 786440 | tf_op jit(solution)/shard_map/ppermute | solution.py:228
  192.7 4.5 %collective-permute-start = (bf16[256,512]{1,0:T(8,128)(2,1)}, bf16[256,512]{1,0:T(8,128)(2,1)}, u32[]{:S(2)}, u32[]{:S(2)}) collective-permute-start(bf16[256,512]{1,0:T(8,128)(2,1)} %bitcast.37), channel_id=1, source_target_pairs={{0,30},{1,31},{2,28},{3,29},{4,26},{5,27},{6,24},{7,25},{8,22},{9,... | collective-permute-start | bytes 786440 | tf_op jit(solution)/shard_map/ppermute | solution.py:228
  207.3 2.2 place.14.refs_4_
  209.5 2.2 place.15.refs_3_
  211.8 2.2 collective-permute-done.1.refs_0_
  214.0 2.0 place.16.refs_1_
  216.0 10.2 %collective-permute-done.refs_0_ = bf16[256,512]{1,0:T(8,128)(2,1)} collective-permute-done((bf16[256,512]{1,0:T(8,128)(2,1)}, bf16[256,512]{1,0:T(8,128)(2,1)}, u32[]{:S(2)}, u32[]{:S(2)}) %collective-permute-start) | collective-permute-done | bytes 262176 | tf_op jit(solution)/shard_map/ppermute | solution.py:228
  (112 shorter events, 73.7 us)
Async XLA Ops:
  2.6 16.9 %collective-permute-start.28 = (bf16[256,512]{1,0:T(8,128)(2,1)}, bf16[256,512]{1,0:T(8,128)(2,1)S(1)}, u32[]{:S(2)}, u32[]{:S(2)}) collective-permute-start(bf16[256,512]{1,0:T(8,128)(2,1)} %bitcast.56), channel_id=1, source_target_pairs={{0,1},{1,0},{2,3},{3,2},{4,5},{5,4},{6,7},{7,6},{8,9},{9,8},{10,11... | collective-permute-start | bytes 786440 | tf_op jit(solution)/shard_map/ppermute | solution.py:228
  7.7 25.1 %collective-permute-start.29 = (bf16[256,512]{1,0:T(8,128)(2,1)}, bf16[256,512]{1,0:T(8,128)(2,1)S(1)}, u32[]{:S(2)}, u32[]{:S(2)}) collective-permute-start(bf16[256,512]{1,0:T(8,128)(2,1)} %bitcast.55), channel_id=1, source_target_pairs={{0,2},{1,3},{2,0},{3,1},{4,6},{5,7},{6,4},{7,5},{8,10},{9,11},{10,... | collective-permute-start | bytes 786440 | tf_op jit(solution)/shard_map/ppermute | solution.py:228
  12.3 20.7 %collective-permute-start.30 = (bf16[256,512]{1,0:T(8,128)(2,1)}, bf16[256,512]{1,0:T(8,128)(2,1)S(1)}, u32[]{:S(2)}, u32[]{:S(2)}) collective-permute-start(bf16[256,512]{1,0:T(8,128)(2,1)} %bitcast.54), channel_id=1, source_target_pairs={{0,3},{1,2},{2,1},{3,0},{4,7},{5,6},{6,5},{7,4},{8,11},{9,10},{10,... | collective-permute-start | bytes 786440 | tf_op jit(solution)/shard_map/ppermute | solution.py:228
  14.4 20.4 %collective-permute-start.24 = (bf16[256,512]{1,0:T(8,128)(2,1)}, bf16[256,512]{1,0:T(8,128)(2,1)S(1)}, u32[]{:S(2)}, u32[]{:S(2)}) collective-permute-start(bf16[256,512]{1,0:T(8,128)(2,1)} %bitcast.53), channel_id=1, source_target_pairs={{0,4},{1,5},{2,6},{3,7},{4,0},{5,1},{6,2},{7,3},{8,12},{9,13},{10,... | collective-permute-start | bytes 786440 | tf_op jit(solution)/shard_map/ppermute | solution.py:228
  16.5 31.7 %collective-permute-start.25 = (bf16[256,512]{1,0:T(8,128)(2,1)}, bf16[256,512]{1,0:T(8,128)(2,1)S(1)}, u32[]{:S(2)}, u32[]{:S(2)}) collective-permute-start(bf16[256,512]{1,0:T(8,128)(2,1)} %bitcast.52), channel_id=1, source_target_pairs={{0,5},{1,4},{2,7},{3,6},{4,1},{5,0},{6,3},{7,2},{8,13},{9,12},{10,... | collective-permute-start | bytes 786440 | tf_op jit(solution)/shard_map/ppermute | solution.py:228
  19.5 29.7 %collective-permute-start.26 = (bf16[256,512]{1,0:T(8,128)(2,1)}, bf16[256,512]{1,0:T(8,128)(2,1)S(1)}, u32[]{:S(2)}, u32[]{:S(2)}) collective-permute-start(bf16[256,512]{1,0:T(8,128)(2,1)} %bitcast.51), channel_id=1, source_target_pairs={{0,6},{1,7},{2,4},{3,5},{4,2},{5,3},{6,0},{7,1},{8,14},{9,15},{10,... | collective-permute-start | bytes 786440 | tf_op jit(solution)/shard_map/ppermute | solution.py:228
  32.9 29.9 %collective-permute-start.27 = (bf16[256,512]{1,0:T(8,128)(2,1)S(1)}, bf16[256,512]{1,0:T(8,128)(2,1)S(1)}, u32[]{:S(2)}, u32[]{:S(2)}) collective-permute-start(bf16[256,512]{1,0:T(8,128)(2,1)S(1)} %bitcast.49), channel_id=1, source_target_pairs={{0,7},{1,6},{2,5},{3,4},{4,3},{5,2},{6,1},{7,0},{8,15},{9,14},{10,... | collective-permute-start | bytes 786440 | tf_op jit(solution)/shard_map/ppermute | solution.py:228
  33.1 34.7 %collective-permute-start.20 = (bf16[256,512]{1,0:T(8,128)(2,1)S(1)}, bf16[256,512]{1,0:T(8,128)(2,1)S(1)}, u32[]{:S(2)}, u32[]{:S(2)}) collective-permute-start(bf16[256,512]{1,0:T(8,128)(2,1)S(1)} %bitcast.46), channel_id=1, source_target_pairs={{0,8},{1,9},{2,10},{3,11},{4,12},{5,13},{6,14},{7,15},{8,0},{9,1},... | collective-permute-start | bytes 786440 | tf_op jit(solution)/shard_map/ppermute | solution.py:228
  34.8 34.9 %collective-permute-start.21 = (bf16[256,512]{1,0:T(8,128)(2,1)S(1)}, bf16[256,512]{1,0:T(8,128)(2,1)S(1)}, u32[]{:S(2)}, u32[]{:S(2)}) collective-permute-start(bf16[256,512]{1,0:T(8,128)(2,1)S(1)} %bitcast.44), channel_id=1, source_target_pairs={{0,9},{1,8},{2,11},{3,10},{4,13},{5,12},{6,15},{7,14},{8,1},{9,0},... | collective-permute-start | bytes 786440 | tf_op jit(solution)/shard_map/ppermute | solution.py:228
  48.2 27.1 %collective-permute-start.22 = (bf16[256,512]{1,0:T(8,128)(2,1)S(1)}, bf16[256,512]{1,0:T(8,128)(2,1)S(1)}, u32[]{:S(2)}, u32[]{:S(2)}) collective-permute-start(bf16[256,512]{1,0:T(8,128)(2,1)S(1)} %bitcast.42), channel_id=1, source_target_pairs={{0,10},{1,11},{2,8},{3,9},{4,14},{5,15},{6,12},{7,13},{8,2},{9,3},... | collective-permute-start | bytes 786440 | tf_op jit(solution)/shard_map/ppermute | solution.py:228
  49.2 26.1 %collective-permute-start.23 = (bf16[256,512]{1,0:T(8,128)(2,1)}, bf16[256,512]{1,0:T(8,128)(2,1)S(1)}, u32[]{:S(2)}, u32[]{:S(2)}) collective-permute-start(bf16[256,512]{1,0:T(8,128)(2,1)} %bitcast.39), channel_id=1, source_target_pairs={{0,11},{1,10},{2,9},{3,8},{4,15},{5,14},{6,13},{7,12},{8,3},{9,2},... | collective-permute-start | bytes 786440 | tf_op jit(solution)/shard_map/ppermute | solution.py:228
  62.7 24.1 %collective-permute-start.16 = (bf16[256,512]{1,0:T(8,128)(2,1)}, bf16[256,512]{1,0:T(8,128)(2,1)S(1)}, u32[]{:S(2)}, u32[]{:S(2)}) collective-permute-start(bf16[256,512]{1,0:T(8,128)(2,1)} %bitcast.16), channel_id=1, source_target_pairs={{0,12},{1,13},{2,14},{3,15},{4,8},{5,9},{6,10},{7,11},{8,4},{9,5},... | collective-permute-start | bytes 786440 | tf_op jit(solution)/shard_map/ppermute | solution.py:228
  67.8 40.7 %collective-permute-start.17 = (bf16[256,512]{1,0:T(8,128)(2,1)S(1)}, bf16[256,512]{1,0:T(8,128)(2,1)S(1)}, u32[]{:S(2)}, u32[]{:S(2)}) collective-permute-start(bf16[256,512]{1,0:T(8,128)(2,1)S(1)} %bitcast.47), channel_id=1, source_target_pairs={{0,13},{1,12},{2,15},{3,14},{4,9},{5,8},{6,11},{7,10},{8,5},{9,4},... | collective-permute-start | bytes 786440 | tf_op jit(solution)/shard_map/ppermute | solution.py:228
  69.7 39.0 %collective-permute-start.18 = (bf16[256,512]{1,0:T(8,128)(2,1)}, bf16[256,512]{1,0:T(8,128)(2,1)S(1)}, u32[]{:S(2)}, u32[]{:S(2)}) collective-permute-start(bf16[256,512]{1,0:T(8,128)(2,1)} %bitcast.18), channel_id=1, source_target_pairs={{0,14},{1,15},{2,12},{3,13},{4,10},{5,11},{6,8},{7,9},{8,6},{9,7},... | collective-permute-start | bytes 786440 | tf_op jit(solution)/shard_map/ppermute | solution.py:228
  75.3 36.6 %collective-permute-start.19 = (bf16[256,512]{1,0:T(8,128)(2,1)}, bf16[256,512]{1,0:T(8,128)(2,1)S(1)}, u32[]{:S(2)}, u32[]{:S(2)}) collective-permute-start(bf16[256,512]{1,0:T(8,128)(2,1)} %bitcast.19), channel_id=1, source_target_pairs={{0,15},{1,14},{2,13},{3,12},{4,11},{5,10},{6,9},{7,8},{8,7},{9,6},... | collective-permute-start | bytes 786440 | tf_op jit(solution)/shard_map/ppermute | solution.py:228
  75.3 38.9 %collective-permute-start.12 = (bf16[256,512]{1,0:T(8,128)(2,1)}, bf16[256,512]{1,0:T(8,128)(2,1)S(1)}, u32[]{:S(2)}, u32[]{:S(2)}) collective-permute-start(bf16[256,512]{1,0:T(8,128)(2,1)} %bitcast.40), channel_id=1, source_target_pairs={{0,16},{1,17},{2,18},{3,19},{4,20},{5,21},{6,22},{7,23},{8,24},{9,... | collective-permute-start | bytes 786440 | tf_op jit(solution)/shard_map/ppermute | solution.py:228
  86.8 39.0 %collective-permute-start.13 = (bf16[256,512]{1,0:T(8,128)(2,1)}, bf16[256,512]{1,0:T(8,128)(2,1)S(1)}, u32[]{:S(2)}, u32[]{:S(2)}) collective-permute-start(bf16[256,512]{1,0:T(8,128)(2,1)} %bitcast.50), channel_id=1, source_target_pairs={{0,17},{1,16},{2,19},{3,18},{4,21},{5,20},{6,23},{7,22},{8,25},{9,... | collective-permute-start | bytes 786440 | tf_op jit(solution)/shard_map/ppermute | solution.py:228
  108.4 29.4 %collective-permute-start.14 = (bf16[256,512]{1,0:T(8,128)(2,1)}, bf16[256,512]{1,0:T(8,128)(2,1)S(1)}, u32[]{:S(2)}, u32[]{:S(2)}) collective-permute-start(bf16[256,512]{1,0:T(8,128)(2,1)} %bitcast.48), channel_id=1, source_target_pairs={{0,18},{1,19},{2,16},{3,17},{4,22},{5,23},{6,20},{7,21},{8,26},{9,... | collective-permute-start | bytes 786440 | tf_op jit(solution)/shard_map/ppermute | solution.py:228
  108.7 29.9 %collective-permute-start.15 = (bf16[256,512]{1,0:T(8,128)(2,1)}, bf16[256,512]{1,0:T(8,128)(2,1)}, u32[]{:S(2)}, u32[]{:S(2)}) collective-permute-start(bf16[256,512]{1,0:T(8,128)(2,1)} %bitcast.45), channel_id=1, source_target_pairs={{0,19},{1,18},{2,17},{3,16},{4,23},{5,22},{6,21},{7,20},{8,27},{9,... | collective-permute-start | bytes 786440 | tf_op jit(solution)/shard_map/ppermute | solution.py:228
  111.9 30.9 %collective-permute-start.10 = (bf16[256,512]{1,0:T(8,128)(2,1)}, bf16[256,512]{1,0:T(8,128)(2,1)}, u32[]{:S(2)}, u32[]{:S(2)}) collective-permute-start(bf16[256,512]{1,0:T(8,128)(2,1)} %bitcast.43), channel_id=1, source_target_pairs={{0,22},{1,23},{2,20},{3,21},{4,18},{5,19},{6,16},{7,17},{8,30},{9,... | collective-permute-start | bytes 786440 | tf_op jit(solution)/shard_map/ppermute | solution.py:228
  114.2 35.9 %collective-permute-start.11 = (bf16[256,512]{1,0:T(8,128)(2,1)}, bf16[256,512]{1,0:T(8,128)(2,1)}, u32[]{:S(2)}, u32[]{:S(2)}) collective-permute-start(bf16[256,512]{1,0:T(8,128)(2,1)} %bitcast.41), channel_id=1, source_target_pairs={{0,23},{1,22},{2,21},{3,20},{4,19},{5,18},{6,17},{7,16},{8,31},{9,... | collective-permute-start | bytes 786440 | tf_op jit(solution)/shard_map/ppermute | solution.py:228
  126.5 58.1 %collective-permute-start.8 = (bf16[256,512]{1,0:T(8,128)(2,1)}, bf16[256,512]{1,0:T(8,128)(2,1)}, u32[]{:S(2)}, u32[]{:S(2)}) collective-permute-start(bf16[256,512]{1,0:T(8,128)(2,1)} %bitcast.8), channel_id=1, source_target_pairs={{0,20},{1,21},{2,22},{3,23},{4,16},{5,17},{6,18},{7,19},{8,28},{9,... | collective-permute-start | bytes 786440 | tf_op jit(solution)/shard_map/ppermute | solution.py:228
  138.6 51.5 %collective-permute-start.9 = (bf16[256,512]{1,0:T(8,128)(2,1)}, bf16[256,512]{1,0:T(8,128)(2,1)}, u32[]{:S(2)}, u32[]{:S(2)}) collective-permute-start(bf16[256,512]{1,0:T(8,128)(2,1)} %bitcast.9), channel_id=1, source_target_pairs={{0,21},{1,20},{2,23},{3,22},{4,17},{5,16},{6,19},{7,18},{8,29},{9,... | collective-permute-start | bytes 786440 | tf_op jit(solution)/shard_map/ppermute | solution.py:228
  138.6 51.5 %collective-permute-start.4 = (bf16[256,512]{1,0:T(8,128)(2,1)}, bf16[256,512]{1,0:T(8,128)(2,1)}, u32[]{:S(2)}, u32[]{:S(2)}) collective-permute-start(bf16[256,512]{1,0:T(8,128)(2,1)} %bitcast.4), channel_id=1, source_target_pairs={{0,24},{1,25},{2,26},{3,27},{4,28},{5,29},{6,30},{7,31},{8,16},{9,... | collective-permute-start | bytes 786440 | tf_op jit(solution)/shard_map/ppermute | solution.py:228
  142.7 49.1 %collective-permute-start.5 = (bf16[256,512]{1,0:T(8,128)(2,1)}, bf16[256,512]{1,0:T(8,128)(2,1)}, u32[]{:S(2)}, u32[]{:S(2)}) collective-permute-start(bf16[256,512]{1,0:T(8,128)(2,1)} %bitcast.5), channel_id=1, source_target_pairs={{0,25},{1,24},{2,27},{3,26},{4,29},{5,28},{6,31},{7,30},{8,17},{9,... | collective-permute-start | bytes 786440 | tf_op jit(solution)/shard_map/ppermute | solution.py:228
  150.1 42.7 %collective-permute-start.6 = (bf16[256,512]{1,0:T(8,128)(2,1)}, bf16[256,512]{1,0:T(8,128)(2,1)}, u32[]{:S(2)}, u32[]{:S(2)}) collective-permute-start(bf16[256,512]{1,0:T(8,128)(2,1)} %bitcast.38), channel_id=1, source_target_pairs={{0,26},{1,27},{2,24},{3,25},{4,30},{5,31},{6,28},{7,29},{8,18},{9,... | collective-permute-start | bytes 786440 | tf_op jit(solution)/shard_map/ppermute | solution.py:228
  167.5 29.7 %all-to-all-start = ((bf16[32,8,128]{2,1,0:T(8,128)(2,1)}), bf16[32,8,128]{2,1,0:T(8,128)(2,1)S(1)}, u32[]{:S(2)}, u32[]{:S(2)}) async-start(bf16[32,8,128]{2,1,0:T(8,128)(2,1)} %bitcast.36), calls=%async_computation | async-start | bytes 131072 | tf_op jit(solution)/shard_map/all_to_all | solution.py:231
  184.6 25.0 %collective-permute-start.7 = (bf16[256,512]{1,0:T(8,128)(2,1)}, bf16[256,512]{1,0:T(8,128)(2,1)}, u32[]{:S(2)}, u32[]{:S(2)}) collective-permute-start(bf16[256,512]{1,0:T(8,128)(2,1)} %bitcast.7), channel_id=1, source_target_pairs={{0,27},{1,26},{2,25},{3,24},{4,31},{5,30},{6,29},{7,28},{8,19},{9,... | collective-permute-start | bytes 786440 | tf_op jit(solution)/shard_map/ppermute | solution.py:228
  190.1 23.9 %collective-permute-start.1 = (bf16[256,512]{1,0:T(8,128)(2,1)}, bf16[256,512]{1,0:T(8,128)(2,1)}, u32[]{:S(2)}, u32[]{:S(2)}) collective-permute-start(bf16[256,512]{1,0:T(8,128)(2,1)} %bitcast.1), channel_id=1, source_target_pairs={{0,28},{1,29},{2,30},{3,31},{4,24},{5,25},{6,26},{7,27},{8,20},{9,... | collective-permute-start | bytes 786440 | tf_op jit(solution)/shard_map/ppermute | solution.py:228
  190.1 23.9 %collective-permute-start.2 = (bf16[256,512]{1,0:T(8,128)(2,1)}, bf16[256,512]{1,0:T(8,128)(2,1)}, u32[]{:S(2)}, u32[]{:S(2)}) collective-permute-start(bf16[256,512]{1,0:T(8,128)(2,1)} %bitcast.2), channel_id=1, source_target_pairs={{0,29},{1,28},{2,31},{3,30},{4,25},{5,24},{6,27},{7,26},{8,21},{9,... | collective-permute-start | bytes 786440 | tf_op jit(solution)/shard_map/ppermute | solution.py:228
  191.8 22.2 %collective-permute-start.3 = (bf16[256,512]{1,0:T(8,128)(2,1)}, bf16[256,512]{1,0:T(8,128)(2,1)}, u32[]{:S(2)}, u32[]{:S(2)}) collective-permute-start(bf16[256,512]{1,0:T(8,128)(2,1)} %bitcast.3), channel_id=1, source_target_pairs={{0,31},{1,30},{2,29},{3,28},{4,27},{5,26},{6,25},{7,24},{8,23},{9,... | collective-permute-start | bytes 786440 | tf_op jit(solution)/shard_map/ppermute | solution.py:228
  192.7 33.5 %collective-permute-start = (bf16[256,512]{1,0:T(8,128)(2,1)}, bf16[256,512]{1,0:T(8,128)(2,1)}, u32[]{:S(2)}, u32[]{:S(2)}) collective-permute-start(bf16[256,512]{1,0:T(8,128)(2,1)} %bitcast.37), channel_id=1, source_target_pairs={{0,30},{1,31},{2,28},{3,29},{4,26},{5,27},{6,24},{7,25},{8,22},{9,... | collective-permute-start | bytes 786440 | tf_op jit(solution)/shard_map/ppermute | solution.py:228
  (18 other events, 126.7 us)
where the time goes:
time: 229 us; the launch traced here: 228 us
  starting transfers between devices  105 us (46%)
  Pallas kernels  86.2 us (38%)
  waiting for transfers between devices  30.4 us (13%)
  local copies, waits for them, and re-layouts  4.7 us (2%)
    ppermute x31, starting transfers between devices, on_device(): block = lax.ppermute(block, AXES, pairs)  99.7 us
    pallas_call x32, Pallas kernels, pack(): pl.pallas_call(functools.partial(pack_kernel, steps, sections_count, rank...  63.7 us
    ppermute x31, waiting for transfers between devices, on_device(): block = lax.ppermute(block, AXES, pairs)  30.4 us
    pallas_call x9, Pallas kernels, place(): pl.pallas_call(functools.partial(place_kernel, steps, sections_count, ran...  14.2 us
    pallas_call x1, Pallas kernels, scales(): pl.pallas_call(scales_kernel, grid=(sections_count,), out_shape=jax.Shape...  8.33 us
    all_to_all x1, starting transfers between devices, on_device(): lax.all_to_all(sent_scales.reshape((sections_count * ranks_count,) + sent...  5.04 us
    unnamed x36, local copies, waits for them, and re-layouts  4.7 us
  transfers between devices with their start and end apart: 32, of which 5 were waited for; matrix products, arithmetic and copies ran while one was open for 0% of the time, Pallas kernels for 36%

commit v1 on v0

--- a/solution.py
+++ b/solution.py
@@ -189,15 +189,20 @@
 
 
 def send_order(sections_count, units_count):
+    sections = list(range(sections_count))
+    if sections_count % 4 == 0:
+        sections = [x for step in range(sections_count // 2) for x in (step, step ^ 3 * sections_count // 4)]
     half = units_count // 2
-    far_steps = [(far, unit) for far in range(sections_count) for unit in reversed(range(half, units_count))]
-    near_steps = [(far, unit) for far in range(sections_count) for unit in reversed(range(half))]
-    near_steps = near_steps[half:] + near_steps[:half]
-    order = far_steps[:2]
-    for index, step in enumerate(far_steps[2:]):
-        order += near_steps[index : index + 1] + [step]
-    rest = near_steps[len(far_steps) - 2 :]
-    return order[:2] + rest[:-1] + order[2:] + rest[-1:]
+    crossing = [(far, unit) for far in sections for unit in reversed(range(half, units_count))]
+    others = [(far, unit) for far in sections for unit in reversed(range(half))]
+    others.remove((0, 0))
+    order = crossing[:2]
+    placed = 0
+    for index, step in enumerate(crossing[2:], 1):
+        until = -(-len(others) * index // (len(crossing) - 2))
+        order += others[placed:until] + [step]
+        placed = until
+    return order + [(0, 0)]
 
 
 def on_device(key_weight, value_weight, norm_gain):

time: 229 us -> 229 us (level)
  waiting for transfers between devices: 30.4 us -> 27.8 us
    all_to_all x1, starting transfers between devices: 5.04 us -> 13.9 us  [on_device(): lax.all_to_all(sent_scales.reshape((sections_count * ranks_count,) + sent...]
    ppermute x31, starting transfers between devices: 99.7 us -> 93.6 us  [on_device(): block = lax.ppermute(block, AXES, pairs)]
    ppermute x31, waiting for transfers between devices: 30.4 us -> 27.8 us  [on_device(): block = lax.ppermute(block, AXES, pairs)]
  transfers between devices with their start and end apart: 32 -> 32, of which waited for: 5 -> 4; matrix products, arithmetic and copies ran while one was open for 0% -> 0% of each run, Pallas kernels for 36% -> 36%
where the time goes in v1:
time: 229 us; the launch traced here: 228 us
  starting transfers between devices  107 us (47%)
  Pallas kernels  86.2 us (38%)
  waiting for transfers between devices  27.8 us (12%)
  local copies, waits for them, and re-layouts  4.69 us (2%)
    ppermute x31, starting transfers between devices, on_device(): block = lax.ppermute(block, AXES, pairs)  93.6 us
    pallas_call x32, Pallas kernels, pack(): pl.pallas_call(functools.partial(pack_kernel, steps, sections_count, rank...  63.7 us
    ppermute x31, waiting for transfers between devices, on_device(): block = lax.ppermute(block, AXES, pairs)  27.8 us
    pallas_call x9, Pallas kernels, place(): pl.pallas_call(functools.partial(place_kernel, steps, sections_count, ran...  14.2 us
    all_to_all x1, starting transfers between devices, on_device(): lax.all_to_all(sent_scales.reshape((sections_count * ranks_count,) + sent...  13.9 us
    pallas_call x1, Pallas kernels, scales(): pl.pallas_call(scales_kernel, grid=(sections_count,), out_shape=jax.Shape...  8.33 us
    unnamed x36, local copies, waits for them, and re-layouts  4.69 us
  transfers between devices with their start and end apart: 32, of which 4 were waited for; matrix products, arithmetic and copies ran while one was open for 0% of the time, Pallas kernels for 36%

profile of v1, /device:TPU:0, one launch (start us, length us, event | category | flops | bytes accessed | tf_op | source)
XLA Modules:
  0.0 228.0 jit_solution(16930351144378203819)
XLA Ops:
  2.6 3.1 %collective-permute-start.28 = (bf16[256,512]{1,0:T(8,128)(2,1)}, bf16[256,512]{1,0:T(8,128)(2,1)S(1)}, u32[]{:S(2)}, u32[]{:S(2)}) collective-permute-start(bf16[256,512]{1,0:T(8,128)(2,1)} %bitcast.56), channel_id=1, source_target_pairs={{0,1},{1,0},{2,3},{3,2},{4,5},{5,4},{6,7},{7,6},{8,9},{9,8},{10,11... | collective-permute-start | bytes 786440 | tf_op jit(solution)/shard_map/ppermute | solution.py:233
  7.7 2.7 %collective-permute-start.29 = (bf16[256,512]{1,0:T(8,128)(2,1)}, bf16[256,512]{1,0:T(8,128)(2,1)S(1)}, u32[]{:S(2)}, u32[]{:S(2)}) collective-permute-start(bf16[256,512]{1,0:T(8,128)(2,1)} %bitcast.55), channel_id=1, source_target_pairs={{0,2},{1,3},{2,0},{3,1},{4,6},{5,7},{6,4},{7,5},{8,10},{9,11},{10,... | collective-permute-start | bytes 786440 | tf_op jit(solution)/shard_map/ppermute | solution.py:233
  14.5 2.0 pack.57
  19.5 3.2 %collective-permute-start.26 = (bf16[256,512]{1,0:T(8,128)(2,1)}, bf16[256,512]{1,0:T(8,128)(2,1)S(1)}, u32[]{:S(2)}, u32[]{:S(2)}) collective-permute-start(bf16[256,512]{1,0:T(8,128)(2,1)} %bitcast.51), channel_id=1, source_target_pairs={{0,6},{1,7},{2,4},{3,5},{4,2},{5,3},{6,0},{7,1},{8,14},{9,15},{10,... | collective-permute-start | bytes 786440 | tf_op jit(solution)/shard_map/ppermute | solution.py:233
  26.7 2.0 pack.53
  28.7 2.1 pack.54
  30.8 2.0 pack.55
  34.8 13.4 %collective-permute-start.21 = (bf16[256,512]{1,0:T(8,128)(2,1)S(1)}, bf16[256,512]{1,0:T(8,128)(2,1)S(1)}, u32[]{:S(2)}, u32[]{:S(2)}) collective-permute-start(bf16[256,512]{1,0:T(8,128)(2,1)S(1)} %bitcast.44), channel_id=1, source_target_pairs={{0,9},{1,8},{2,11},{3,10},{4,13},{5,12},{6,15},{7,14},{8,1},{9,0},... | collective-permute-start | bytes 786440 | tf_op jit(solution)/shard_map/ppermute | solution.py:233
  49.2 3.5 %collective-permute-start.23 = (bf16[256,512]{1,0:T(8,128)(2,1)}, bf16[256,512]{1,0:T(8,128)(2,1)S(1)}, u32[]{:S(2)}, u32[]{:S(2)}) collective-permute-start(bf16[256,512]{1,0:T(8,128)(2,1)} %bitcast.39), channel_id=1, source_target_pairs={{0,11},{1,10},{2,9},{3,8},{4,15},{5,14},{6,13},{7,12},{8,3},{9,2},... | collective-permute-start | bytes 786440 | tf_op jit(solution)/shard_map/ppermute | solution.py:233
  58.7 2.1 pack.51
  62.7 5.0 %collective-permute-start.16 = (bf16[256,512]{1,0:T(8,128)(2,1)}, bf16[256,512]{1,0:T(8,128)(2,1)S(1)}, u32[]{:S(2)}, u32[]{:S(2)}) collective-permute-start(bf16[256,512]{1,0:T(8,128)(2,1)} %bitcast.16), channel_id=1, source_target_pairs={{0,12},{1,13},{2,14},{3,15},{4,8},{5,9},{6,10},{7,11},{8,4},{9,5},... | collective-permute-start | bytes 786440 | tf_op jit(solution)/shard_map/ppermute | solution.py:233
  70.7 4.6 %collective-permute-done.22.refs_2_ = bf16[256,512]{1,0:T(8,128)(2,1)S(1)} collective-permute-done((bf16[256,512]{1,0:T(8,128)(2,1)S(1)}, bf16[256,512]{1,0:T(8,128)(2,1)S(1)}, u32[]{:S(2)}, u32[]{:S(2)}) %collective-permute-start.22) | collective-permute-done | bytes 262176 | tf_op jit(solution)/shard_map/ppermute | solution.py:233
  78.8 2.0 pack.46
  86.8 21.6 %collective-permute-start.13 = (bf16[256,512]{1,0:T(8,128)(2,1)}, bf16[256,512]{1,0:T(8,128)(2,1)S(1)}, u32[]{:S(2)}, u32[]{:S(2)}) collective-permute-start(bf16[256,512]{1,0:T(8,128)(2,1)} %bitcast.50), channel_id=1, source_target_pairs={{0,17},{1,16},{2,19},{3,18},{4,21},{5,20},{6,23},{7,22},{8,25},{9,... | collective-permute-start | bytes 786440 | tf_op jit(solution)/shard_map/ppermute | solution.py:233
  108.7 3.2 %collective-permute-start.15 = (bf16[256,512]{1,0:T(8,128)(2,1)}, bf16[256,512]{1,0:T(8,128)(2,1)}, u32[]{:S(2)}, u32[]{:S(2)}) collective-permute-start(bf16[256,512]{1,0:T(8,128)(2,1)} %bitcast.45), channel_id=1, source_target_pairs={{0,19},{1,18},{2,17},{3,16},{4,23},{5,22},{6,21},{7,20},{8,27},{9,... | collective-permute-start | bytes 786440 | tf_op jit(solution)/shard_map/ppermute | solution.py:233
  111.8 2.7 %collective-permute-start.10 = (bf16[256,512]{1,0:T(8,128)(2,1)}, bf16[256,512]{1,0:T(8,128)(2,1)}, u32[]{:S(2)}, u32[]{:S(2)}) collective-permute-start(bf16[256,512]{1,0:T(8,128)(2,1)} %bitcast.43), channel_id=1, source_target_pairs={{0,21},{1,20},{2,23},{3,22},{4,17},{5,16},{6,19},{7,18},{8,29},{9,... | collective-permute-start | bytes 786440 | tf_op jit(solution)/shard_map/ppermute | solution.py:233
  121.1 2.0 pack.39
  127.5 6.8 %collective-permute-done.14.refs_2_ = bf16[256,512]{1,0:T(8,128)(2,1)S(1)} collective-permute-done((bf16[256,512]{1,0:T(8,128)(2,1)}, bf16[256,512]{1,0:T(8,128)(2,1)S(1)}, u32[]{:S(2)}, u32[]{:S(2)}) %collective-permute-start.14) | collective-permute-done | bytes 262176 | tf_op jit(solution)/shard_map/ppermute | solution.py:233
  135.0 6.7 %collective-permute-start.6 = (bf16[256,512]{1,0:T(8,128)(2,1)}, bf16[256,512]{1,0:T(8,128)(2,1)}, u32[]{:S(2)}, u32[]{:S(2)}) collective-permute-start(bf16[256,512]{1,0:T(8,128)(2,1)} %bitcast.6), channel_id=1, source_target_pairs={{0,25},{1,24},{2,27},{3,26},{4,29},{5,28},{6,31},{7,30},{8,17},{9,... | collective-permute-start | bytes 786440 | tf_op jit(solution)/shard_map/ppermute | solution.py:233
  141.7 2.1 collective-permute-start.7
  143.8 4.9 %collective-permute-start.8 = (bf16[256,512]{1,0:T(8,128)(2,1)}, bf16[256,512]{1,0:T(8,128)(2,1)}, u32[]{:S(2)}, u32[]{:S(2)}) collective-permute-start(bf16[256,512]{1,0:T(8,128)(2,1)} %bitcast.38), channel_id=1, source_target_pairs={{0,27},{1,26},{2,25},{3,24},{4,31},{5,30},{6,29},{7,28},{8,19},{9,... | collective-permute-start | bytes 786440 | tf_op jit(solution)/shard_map/ppermute | solution.py:233
  148.7 8.3 %scales.1 = bf16[8,4,8,128]{3,2,1,0:T(8,128)(2,1)} custom-call(bf16[1,8192,256]{2,1,0:T(8,128)(2,1)} %key_ref.65, bf16[1,8192,256]{2,1,0:T(8,128)(2,1)} %value_ref.65, bf16[1,8192]{1,0:T(2,128)(2,1)} %gain_ref.65), custom_call_target="tpu_custom_call" | custom-call | flops 41943040 | bytes 8388608 | tf_op jit(solution)/shard_map/scales/pallas_call | solution.py:175
  157.0 13.9 %all-to-all-start = ((bf16[32,8,128]{2,1,0:T(8,128)(2,1)}), bf16[32,8,128]{2,1,0:T(8,128)(2,1)S(1)}, u32[]{:S(2)}, u32[]{:S(2)}) async-start(bf16[32,8,128]{2,1,0:T(8,128)(2,1)} %bitcast.36), calls=%async_computation | async-start | bytes 131072 | tf_op jit(solution)/shard_map/all_to_all | solution.py:236
  178.9 2.0 pack.36
  182.9 2.5 %collective-permute-start.1 = (bf16[256,512]{1,0:T(8,128)(2,1)}, bf16[256,512]{1,0:T(8,128)(2,1)}, u32[]{:S(2)}, u32[]{:S(2)}) collective-permute-start(bf16[256,512]{1,0:T(8,128)(2,1)} %bitcast.1), channel_id=1, source_target_pairs={{0,28},{1,29},{2,30},{3,31},{4,24},{5,25},{6,26},{7,27},{8,20},{9,... | collective-permute-start | bytes 786440 | tf_op jit(solution)/shard_map/ppermute | solution.py:233
  186.9 4.0 %collective-permute-start.3 = (bf16[256,512]{1,0:T(8,128)(2,1)}, bf16[256,512]{1,0:T(8,128)(2,1)}, u32[]{:S(2)}, u32[]{:S(2)}) collective-permute-start(bf16[256,512]{1,0:T(8,128)(2,1)} %bitcast.3), channel_id=1, source_target_pairs={{0,30},{1,31},{2,28},{3,29},{4,26},{5,27},{6,24},{7,25},{8,22},{9,... | collective-permute-start | bytes 786440 | tf_op jit(solution)/shard_map/ppermute | solution.py:233
  191.0 2.4 %collective-permute-start = (bf16[256,512]{1,0:T(8,128)(2,1)}, bf16[256,512]{1,0:T(8,128)(2,1)}, u32[]{:S(2)}, u32[]{:S(2)}) collective-permute-start(bf16[256,512]{1,0:T(8,128)(2,1)} %bitcast.37), channel_id=1, source_target_pairs={{0,22},{1,23},{2,20},{3,21},{4,18},{5,19},{6,16},{7,17},{8,30},{9,... | collective-permute-start | bytes 786440 | tf_op jit(solution)/shard_map/ppermute | solution.py:233
  203.5 2.0 place.14.refs_4_
  205.6 2.2 place.15.refs_4_
  207.8 7.3 %collective-permute-done.3.refs_2_ = bf16[256,512]{1,0:T(8,128)(2,1)} collective-permute-done((bf16[256,512]{1,0:T(8,128)(2,1)}, bf16[256,512]{1,0:T(8,128)(2,1)}, u32[]{:S(2)}, u32[]{:S(2)}) %collective-permute-start.3) | collective-permute-done | bytes 262176 | tf_op jit(solution)/shard_map/ppermute | solution.py:233
  215.1 2.2 place.16.refs_1_
  217.3 9.0 %collective-permute-done.refs_0_ = bf16[256,512]{1,0:T(8,128)(2,1)} collective-permute-done((bf16[256,512]{1,0:T(8,128)(2,1)}, bf16[256,512]{1,0:T(8,128)(2,1)}, u32[]{:S(2)}, u32[]{:S(2)}) %collective-permute-start) | collective-permute-done | bytes 262176 | tf_op jit(solution)/shard_map/ppermute | solution.py:233
  (112 shorter events, 73.3 us)
Async XLA Ops:
  2.6 16.9 %collective-permute-start.28 = (bf16[256,512]{1,0:T(8,128)(2,1)}, bf16[256,512]{1,0:T(8,128)(2,1)S(1)}, u32[]{:S(2)}, u32[]{:S(2)}) collective-permute-start(bf16[256,512]{1,0:T(8,128)(2,1)} %bitcast.56), channel_id=1, source_target_pairs={{0,1},{1,0},{2,3},{3,2},{4,5},{5,4},{6,7},{7,6},{8,9},{9,8},{10,11... | collective-permute-start | bytes 786440 | tf_op jit(solution)/shard_map/ppermute | solution.py:233
  7.7 25.1 %collective-permute-start.29 = (bf16[256,512]{1,0:T(8,128)(2,1)}, bf16[256,512]{1,0:T(8,128)(2,1)S(1)}, u32[]{:S(2)}, u32[]{:S(2)}) collective-permute-start(bf16[256,512]{1,0:T(8,128)(2,1)} %bitcast.55), channel_id=1, source_target_pairs={{0,2},{1,3},{2,0},{3,1},{4,6},{5,7},{6,4},{7,5},{8,10},{9,11},{10,... | collective-permute-start | bytes 786440 | tf_op jit(solution)/shard_map/ppermute | solution.py:233
  12.3 20.7 %collective-permute-start.30 = (bf16[256,512]{1,0:T(8,128)(2,1)}, bf16[256,512]{1,0:T(8,128)(2,1)S(1)}, u32[]{:S(2)}, u32[]{:S(2)}) collective-permute-start(bf16[256,512]{1,0:T(8,128)(2,1)} %bitcast.54), channel_id=1, source_target_pairs={{0,3},{1,2},{2,1},{3,0},{4,7},{5,6},{6,5},{7,4},{8,11},{9,10},{10,... | collective-permute-start | bytes 786440 | tf_op jit(solution)/shard_map/ppermute | solution.py:233
  14.4 20.4 %collective-permute-start.24 = (bf16[256,512]{1,0:T(8,128)(2,1)}, bf16[256,512]{1,0:T(8,128)(2,1)S(1)}, u32[]{:S(2)}, u32[]{:S(2)}) collective-permute-start(bf16[256,512]{1,0:T(8,128)(2,1)} %bitcast.53), channel_id=1, source_target_pairs={{0,4},{1,5},{2,6},{3,7},{4,0},{5,1},{6,2},{7,3},{8,12},{9,13},{10,... | collective-permute-start | bytes 786440 | tf_op jit(solution)/shard_map/ppermute | solution.py:233
  16.5 31.7 %collective-permute-start.25 = (bf16[256,512]{1,0:T(8,128)(2,1)}, bf16[256,512]{1,0:T(8,128)(2,1)S(1)}, u32[]{:S(2)}, u32[]{:S(2)}) collective-permute-start(bf16[256,512]{1,0:T(8,128)(2,1)} %bitcast.52), channel_id=1, source_target_pairs={{0,5},{1,4},{2,7},{3,6},{4,1},{5,0},{6,3},{7,2},{8,13},{9,12},{10,... | collective-permute-start | bytes 786440 | tf_op jit(solution)/shard_map/ppermute | solution.py:233
  19.5 29.7 %collective-permute-start.26 = (bf16[256,512]{1,0:T(8,128)(2,1)}, bf16[256,512]{1,0:T(8,128)(2,1)S(1)}, u32[]{:S(2)}, u32[]{:S(2)}) collective-permute-start(bf16[256,512]{1,0:T(8,128)(2,1)} %bitcast.51), channel_id=1, source_target_pairs={{0,6},{1,7},{2,4},{3,5},{4,2},{5,3},{6,0},{7,1},{8,14},{9,15},{10,... | collective-permute-start | bytes 786440 | tf_op jit(solution)/shard_map/ppermute | solution.py:233
  32.9 29.9 %collective-permute-start.27 = (bf16[256,512]{1,0:T(8,128)(2,1)S(1)}, bf16[256,512]{1,0:T(8,128)(2,1)S(1)}, u32[]{:S(2)}, u32[]{:S(2)}) collective-permute-start(bf16[256,512]{1,0:T(8,128)(2,1)S(1)} %bitcast.49), channel_id=1, source_target_pairs={{0,7},{1,6},{2,5},{3,4},{4,3},{5,2},{6,1},{7,0},{8,15},{9,14},{10,... | collective-permute-start | bytes 786440 | tf_op jit(solution)/shard_map/ppermute | solution.py:233
  33.1 34.7 %collective-permute-start.20 = (bf16[256,512]{1,0:T(8,128)(2,1)S(1)}, bf16[256,512]{1,0:T(8,128)(2,1)S(1)}, u32[]{:S(2)}, u32[]{:S(2)}) collective-permute-start(bf16[256,512]{1,0:T(8,128)(2,1)S(1)} %bitcast.46), channel_id=1, source_target_pairs={{0,8},{1,9},{2,10},{3,11},{4,12},{5,13},{6,14},{7,15},{8,0},{9,1},... | collective-permute-start | bytes 786440 | tf_op jit(solution)/shard_map/ppermute | solution.py:233
  34.8 34.9 %collective-permute-start.21 = (bf16[256,512]{1,0:T(8,128)(2,1)S(1)}, bf16[256,512]{1,0:T(8,128)(2,1)S(1)}, u32[]{:S(2)}, u32[]{:S(2)}) collective-permute-start(bf16[256,512]{1,0:T(8,128)(2,1)S(1)} %bitcast.44), channel_id=1, source_target_pairs={{0,9},{1,8},{2,11},{3,10},{4,13},{5,12},{6,15},{7,14},{8,1},{9,0},... | collective-permute-start | bytes 786440 | tf_op jit(solution)/shard_map/ppermute | solution.py:233
  48.2 27.1 %collective-permute-start.22 = (bf16[256,512]{1,0:T(8,128)(2,1)S(1)}, bf16[256,512]{1,0:T(8,128)(2,1)S(1)}, u32[]{:S(2)}, u32[]{:S(2)}) collective-permute-start(bf16[256,512]{1,0:T(8,128)(2,1)S(1)} %bitcast.42), channel_id=1, source_target_pairs={{0,10},{1,11},{2,8},{3,9},{4,14},{5,15},{6,12},{7,13},{8,2},{9,3},... | collective-permute-start | bytes 786440 | tf_op jit(solution)/shard_map/ppermute | solution.py:233
  49.2 26.1 %collective-permute-start.23 = (bf16[256,512]{1,0:T(8,128)(2,1)}, bf16[256,512]{1,0:T(8,128)(2,1)S(1)}, u32[]{:S(2)}, u32[]{:S(2)}) collective-permute-start(bf16[256,512]{1,0:T(8,128)(2,1)} %bitcast.39), channel_id=1, source_target_pairs={{0,11},{1,10},{2,9},{3,8},{4,15},{5,14},{6,13},{7,12},{8,3},{9,2},... | collective-permute-start | bytes 786440 | tf_op jit(solution)/shard_map/ppermute | solution.py:233
  62.7 24.0 %collective-permute-start.16 = (bf16[256,512]{1,0:T(8,128)(2,1)}, bf16[256,512]{1,0:T(8,128)(2,1)S(1)}, u32[]{:S(2)}, u32[]{:S(2)}) collective-permute-start(bf16[256,512]{1,0:T(8,128)(2,1)} %bitcast.16), channel_id=1, source_target_pairs={{0,12},{1,13},{2,14},{3,15},{4,8},{5,9},{6,10},{7,11},{8,4},{9,5},... | collective-permute-start | bytes 786440 | tf_op jit(solution)/shard_map/ppermute | solution.py:233
  67.8 40.7 %collective-permute-start.17 = (bf16[256,512]{1,0:T(8,128)(2,1)S(1)}, bf16[256,512]{1,0:T(8,128)(2,1)S(1)}, u32[]{:S(2)}, u32[]{:S(2)}) collective-permute-start(bf16[256,512]{1,0:T(8,128)(2,1)S(1)} %bitcast.47), channel_id=1, source_target_pairs={{0,13},{1,12},{2,15},{3,14},{4,9},{5,8},{6,11},{7,10},{8,5},{9,4},... | collective-permute-start | bytes 786440 | tf_op jit(solution)/shard_map/ppermute | solution.py:233
  69.7 39.0 %collective-permute-start.18 = (bf16[256,512]{1,0:T(8,128)(2,1)}, bf16[256,512]{1,0:T(8,128)(2,1)S(1)}, u32[]{:S(2)}, u32[]{:S(2)}) collective-permute-start(bf16[256,512]{1,0:T(8,128)(2,1)} %bitcast.18), channel_id=1, source_target_pairs={{0,14},{1,15},{2,12},{3,13},{4,10},{5,11},{6,8},{7,9},{8,6},{9,7},... | collective-permute-start | bytes 786440 | tf_op jit(solution)/shard_map/ppermute | solution.py:233
  75.3 36.5 %collective-permute-start.19 = (bf16[256,512]{1,0:T(8,128)(2,1)}, bf16[256,512]{1,0:T(8,128)(2,1)S(1)}, u32[]{:S(2)}, u32[]{:S(2)}) collective-permute-start(bf16[256,512]{1,0:T(8,128)(2,1)} %bitcast.19), channel_id=1, source_target_pairs={{0,15},{1,14},{2,13},{3,12},{4,11},{5,10},{6,9},{7,8},{8,7},{9,6},... | collective-permute-start | bytes 786440 | tf_op jit(solution)/shard_map/ppermute | solution.py:233
  75.3 39.2 %collective-permute-start.12 = (bf16[256,512]{1,0:T(8,128)(2,1)}, bf16[256,512]{1,0:T(8,128)(2,1)S(1)}, u32[]{:S(2)}, u32[]{:S(2)}) collective-permute-start(bf16[256,512]{1,0:T(8,128)(2,1)} %bitcast.40), channel_id=1, source_target_pairs={{0,16},{1,17},{2,18},{3,19},{4,20},{5,21},{6,22},{7,23},{8,24},{9,... | collective-permute-start | bytes 786440 | tf_op jit(solution)/shard_map/ppermute | solution.py:233
  86.8 38.3 %collective-permute-start.13 = (bf16[256,512]{1,0:T(8,128)(2,1)}, bf16[256,512]{1,0:T(8,128)(2,1)S(1)}, u32[]{:S(2)}, u32[]{:S(2)}) collective-permute-start(bf16[256,512]{1,0:T(8,128)(2,1)} %bitcast.50), channel_id=1, source_target_pairs={{0,17},{1,16},{2,19},{3,18},{4,21},{5,20},{6,23},{7,22},{8,25},{9,... | collective-permute-start | bytes 786440 | tf_op jit(solution)/shard_map/ppermute | solution.py:233
  108.4 25.8 %collective-permute-start.14 = (bf16[256,512]{1,0:T(8,128)(2,1)}, bf16[256,512]{1,0:T(8,128)(2,1)S(1)}, u32[]{:S(2)}, u32[]{:S(2)}) collective-permute-start(bf16[256,512]{1,0:T(8,128)(2,1)} %bitcast.48), channel_id=1, source_target_pairs={{0,18},{1,19},{2,16},{3,17},{4,22},{5,23},{6,20},{7,21},{8,26},{9,... | collective-permute-start | bytes 786440 | tf_op jit(solution)/shard_map/ppermute | solution.py:233
  108.7 26.3 %collective-permute-start.15 = (bf16[256,512]{1,0:T(8,128)(2,1)}, bf16[256,512]{1,0:T(8,128)(2,1)}, u32[]{:S(2)}, u32[]{:S(2)}) collective-permute-start(bf16[256,512]{1,0:T(8,128)(2,1)} %bitcast.45), channel_id=1, source_target_pairs={{0,19},{1,18},{2,17},{3,16},{4,23},{5,22},{6,21},{7,20},{8,27},{9,... | collective-permute-start | bytes 786440 | tf_op jit(solution)/shard_map/ppermute | solution.py:233
  111.8 29.9 %collective-permute-start.10 = (bf16[256,512]{1,0:T(8,128)(2,1)}, bf16[256,512]{1,0:T(8,128)(2,1)}, u32[]{:S(2)}, u32[]{:S(2)}) collective-permute-start(bf16[256,512]{1,0:T(8,128)(2,1)} %bitcast.43), channel_id=1, source_target_pairs={{0,21},{1,20},{2,23},{3,22},{4,17},{5,16},{6,19},{7,18},{8,29},{9,... | collective-permute-start | bytes 786440 | tf_op jit(solution)/shard_map/ppermute | solution.py:233
  114.5 29.3 %collective-permute-start.11 = (bf16[256,512]{1,0:T(8,128)(2,1)}, bf16[256,512]{1,0:T(8,128)(2,1)}, u32[]{:S(2)}, u32[]{:S(2)}) collective-permute-start(bf16[256,512]{1,0:T(8,128)(2,1)} %bitcast.41), channel_id=1, source_target_pairs={{0,23},{1,22},{2,21},{3,20},{4,19},{5,18},{6,17},{7,16},{8,31},{9,... | collective-permute-start | bytes 786440 | tf_op jit(solution)/shard_map/ppermute | solution.py:233
  125.8 57.2 %collective-permute-start.9 = (bf16[256,512]{1,0:T(8,128)(2,1)}, bf16[256,512]{1,0:T(8,128)(2,1)}, u32[]{:S(2)}, u32[]{:S(2)}) collective-permute-start(bf16[256,512]{1,0:T(8,128)(2,1)} %bitcast.9), channel_id=1, source_target_pairs={{0,20},{1,21},{2,22},{3,23},{4,16},{5,17},{6,18},{7,19},{8,28},{9,... | collective-permute-start | bytes 786440 | tf_op jit(solution)/shard_map/ppermute | solution.py:233
  135.0 50.4 %collective-permute-start.5 = (bf16[256,512]{1,0:T(8,128)(2,1)}, bf16[256,512]{1,0:T(8,128)(2,1)}, u32[]{:S(2)}, u32[]{:S(2)}) collective-permute-start(bf16[256,512]{1,0:T(8,128)(2,1)} %bitcast.5), channel_id=1, source_target_pairs={{0,24},{1,25},{2,26},{3,27},{4,28},{5,29},{6,30},{7,31},{8,16},{9,... | collective-permute-start | bytes 786440 | tf_op jit(solution)/shard_map/ppermute | solution.py:233
  135.0 51.9 %collective-permute-start.6 = (bf16[256,512]{1,0:T(8,128)(2,1)}, bf16[256,512]{1,0:T(8,128)(2,1)}, u32[]{:S(2)}, u32[]{:S(2)}) collective-permute-start(bf16[256,512]{1,0:T(8,128)(2,1)} %bitcast.6), channel_id=1, source_target_pairs={{0,25},{1,24},{2,27},{3,26},{4,29},{5,28},{6,31},{7,30},{8,17},{9,... | collective-permute-start | bytes 786440 | tf_op jit(solution)/shard_map/ppermute | solution.py:233
  141.7 49.2 %collective-permute-start.7 = (bf16[256,512]{1,0:T(8,128)(2,1)}, bf16[256,512]{1,0:T(8,128)(2,1)}, u32[]{:S(2)}, u32[]{:S(2)}) collective-permute-start(bf16[256,512]{1,0:T(8,128)(2,1)} %bitcast.7), channel_id=1, source_target_pairs={{0,26},{1,27},{2,24},{3,25},{4,30},{5,31},{6,28},{7,29},{8,18},{9,... | collective-permute-start | bytes 786440 | tf_op jit(solution)/shard_map/ppermute | solution.py:233
  143.8 47.2 %collective-permute-start.8 = (bf16[256,512]{1,0:T(8,128)(2,1)}, bf16[256,512]{1,0:T(8,128)(2,1)}, u32[]{:S(2)}, u32[]{:S(2)}) collective-permute-start(bf16[256,512]{1,0:T(8,128)(2,1)} %bitcast.38), channel_id=1, source_target_pairs={{0,27},{1,26},{2,25},{3,24},{4,31},{5,30},{6,29},{7,28},{8,19},{9,... | collective-permute-start | bytes 786440 | tf_op jit(solution)/shard_map/ppermute | solution.py:233
  157.0 36.4 %all-to-all-start = ((bf16[32,8,128]{2,1,0:T(8,128)(2,1)}), bf16[32,8,128]{2,1,0:T(8,128)(2,1)S(1)}, u32[]{:S(2)}, u32[]{:S(2)}) async-start(bf16[32,8,128]{2,1,0:T(8,128)(2,1)} %bitcast.36), calls=%async_computation | async-start | bytes 131072 | tf_op jit(solution)/shard_map/all_to_all | solution.py:236
  182.9 24.8 %collective-permute-start.1 = (bf16[256,512]{1,0:T(8,128)(2,1)}, bf16[256,512]{1,0:T(8,128)(2,1)}, u32[]{:S(2)}, u32[]{:S(2)}) collective-permute-start(bf16[256,512]{1,0:T(8,128)(2,1)} %bitcast.1), channel_id=1, source_target_pairs={{0,28},{1,29},{2,30},{3,31},{4,24},{5,25},{6,26},{7,27},{8,20},{9,... | collective-permute-start | bytes 786440 | tf_op jit(solution)/shard_map/ppermute | solution.py:233
  185.4 22.4 %collective-permute-start.2 = (bf16[256,512]{1,0:T(8,128)(2,1)}, bf16[256,512]{1,0:T(8,128)(2,1)}, u32[]{:S(2)}, u32[]{:S(2)}) collective-permute-start(bf16[256,512]{1,0:T(8,128)(2,1)} %bitcast.2), channel_id=1, source_target_pairs={{0,29},{1,28},{2,31},{3,30},{4,25},{5,24},{6,27},{7,26},{8,21},{9,... | collective-permute-start | bytes 786440 | tf_op jit(solution)/shard_map/ppermute | solution.py:233
  186.9 28.2 %collective-permute-start.3 = (bf16[256,512]{1,0:T(8,128)(2,1)}, bf16[256,512]{1,0:T(8,128)(2,1)}, u32[]{:S(2)}, u32[]{:S(2)}) collective-permute-start(bf16[256,512]{1,0:T(8,128)(2,1)} %bitcast.3), channel_id=1, source_target_pairs={{0,30},{1,31},{2,28},{3,29},{4,26},{5,27},{6,24},{7,25},{8,22},{9,... | collective-permute-start | bytes 786440 | tf_op jit(solution)/shard_map/ppermute | solution.py:233
  190.9 24.2 %collective-permute-start.4 = (bf16[256,512]{1,0:T(8,128)(2,1)}, bf16[256,512]{1,0:T(8,128)(2,1)}, u32[]{:S(2)}, u32[]{:S(2)}) collective-permute-start(bf16[256,512]{1,0:T(8,128)(2,1)} %bitcast.4), channel_id=1, source_target_pairs={{0,31},{1,30},{2,29},{3,28},{4,27},{5,26},{6,25},{7,24},{8,23},{9,... | collective-permute-start | bytes 786440 | tf_op jit(solution)/shard_map/ppermute | solution.py:233
  191.0 35.3 %collective-permute-start = (bf16[256,512]{1,0:T(8,128)(2,1)}, bf16[256,512]{1,0:T(8,128)(2,1)}, u32[]{:S(2)}, u32[]{:S(2)}) collective-permute-start(bf16[256,512]{1,0:T(8,128)(2,1)} %bitcast.37), channel_id=1, source_target_pairs={{0,22},{1,23},{2,20},{3,21},{4,18},{5,19},{6,16},{7,17},{8,30},{9,... | collective-permute-start | bytes 786440 | tf_op jit(solution)/shard_map/ppermute | solution.py:233
  (18 other events, 122.8 us)
